TPU v7x, 32 devices: a whole 2x2x4 slice. The times are simulated.
32 devices in a mesh: dp: 16 (over z, y, x), feat: 2 (over core).
Axes of the slice: x: 2, y: 2, z: 4, core: 2. Of those that a mesh axis runs over, the one named last changes fastest.
Arguments:
- samples: bfloat16 [4096, 16384], P('dp', 'feat'), may hold values from -1 to 1
- labels: int32 [4096], P('dp'), may hold values from -1 to 1, as said below
- dual: float32 [4096], P('dp'), may hold values from 0 to 1
- counts: int32 [16], P('dp'), may hold values from 1 to 2, as said below
- order: int32 [16, 2], P('dp'), may hold values from 0 to 1, each once within a row
- weights: float32 [16384], P('feat'), may hold values from -0.046875 to 0.046875
Outputs:
- weights_new: float32 [16384], P('feat')
- dual_new: float32 [4096], P('dp')
- margins: float32 [4096], P('dp')
- gap: float32 [], replicated
Inputs may be any that keep to these rules, and one draw needn't show every extreme that they name: `labels`: each entry is -1 or 1. `counts`: some index of dp has exactly 2 live blocks.
All inputs are finite; a program needn't handle non-finite values.
Results may differ from a plain program's by a relative error of at most 0.003.
Values sent between devices are 32-bit elements; how exact they have to be, the bound alone decides.
A program may use at most 64 MiB of HBM per device.

v0:
```python
import jax
import jax.numpy as jnp
from jax import lax
from jax.sharding import PartitionSpec as P

BLOCK = 128
CAP = 2
PASSES = 2


def block_solve(system, right):
    factor = jnp.linalg.cholesky(system)
    lower_part = lax.linalg.triangular_solve(factor, right[:, None], left_side=True, lower=True)
    result = lax.linalg.triangular_solve(
        factor, lower_part, left_side=True, lower=True, transpose_a=True
    )
    return result[:, 0]


def body(samples, labels, dual, counts, order, weights):
    reg = 1.0 / 384.0
    groups = lax.axis_size("dp")
    half = samples.shape[1]
    blocks_x = samples.reshape(CAP, BLOCK, half)
    total = lax.psum(counts[0].astype(jnp.float32), "dp") * BLOCK
    scale = groups / (reg * total)
    count = counts[0]
    partial_grams = jnp.einsum(
        "brd,bsd->brs", blocks_x, blocks_x, preferred_element_type=jnp.float32
    )
    grams = lax.psum(partial_grams, "feat")

    def advance(step, carry):
        beta, change = carry
        slot = order[0, step % CAP]
        rows = lax.dynamic_index_in_dim(blocks_x, slot, 0, keepdims=False)
        vector = (weights + change).astype(jnp.bfloat16)
        partial_margin = jnp.dot(rows, vector, preferred_element_type=jnp.float32)
        margin = lax.psum(partial_margin, "feat")
        gram = lax.dynamic_index_in_dim(grams, slot, 0, keepdims=False)
        start = slot * BLOCK
        signs = lax.dynamic_slice_in_dim(labels, start, BLOCK).astype(jnp.float32)
        before = lax.dynamic_slice_in_dim(beta, start, BLOCK)
        system = (
            jnp.eye(BLOCK, dtype=jnp.float32) + scale * (signs[:, None] * signs[None, :]) * gram
        )
        delta = block_solve(system, 1.0 - before - signs * margin)
        after = jnp.where(slot < count, jnp.maximum(before + delta, 0.0), before)
        scaled = (signs * (after - before)).astype(jnp.bfloat16)
        change = change + scale * jnp.dot(scaled, rows, preferred_element_type=jnp.float32)
        beta = lax.dynamic_update_slice_in_dim(beta, after, start, 0)
        return (beta, change)

    beta, change = lax.fori_loop(0, PASSES * CAP, advance, (dual, jnp.zeros((half,), jnp.float32)))
    summed = lax.psum(change, "dp")
    weights_new = weights + summed / groups
    first_group = (lax.axis_index("dp") == 0).astype(jnp.float32)
    norm_part = jnp.sum(weights_new * weights_new) * first_group
    partial_scores = jnp.dot(
        samples, weights_new.astype(jnp.bfloat16), preferred_element_type=jnp.float32
    )
    margins = lax.psum(partial_scores, "feat")
    slots = jnp.arange(CAP * BLOCK, dtype=jnp.int32)
    live = slots // BLOCK < count
    signs = labels.astype(jnp.float32)
    hinge = jnp.maximum(1.0 - signs * margins, 0.0)
    first_half = (lax.axis_index("feat") == 0).astype(jnp.float32)
    loss_part = jnp.sum(jnp.where(live, 0.5 * hinge * hinge, 0.0)) * first_half
    dual_part = jnp.sum(jnp.where(live, beta - 0.5 * beta * beta, 0.0)) * first_half
    loss, dualsum, norm = lax.psum((loss_part, dual_part, norm_part), ("dp", "feat"))
    gap = reg * norm + (loss - dualsum) / total
    return (weights_new, beta, margins, gap)


def solution(mesh):
    return jax.shard_map(
        body,
        mesh=mesh,
        in_specs=(P("dp", "feat"), P("dp"), P("dp"), P("dp"), P("dp", None), P("feat")),
        out_specs=(P("feat"), P("dp"), P("dp"), P()),
        check_vma=False,
    )
```

profile of v0, /device:TPU:12, one launch (start us, length us, event | category | flops | bytes accessed | tf_op | source)
XLA Modules:
  0.0 335.4 jit_solution(18046364474905601856)
XLA Ops:
  7.3 5.4 %fusion.36 = f32[2,128,128]{2,1,0:T(8,128)} fusion(bf16[2,128,8192]{2,1,0:T(8,128)(2,1)} %bitcast.91), kind=kOutput, calls=%fused_computation.55 | convolution fusion | flops 536870912 | bytes 4325376 | tf_op jit(solution)/shard_map/brd,bsd->brs/dot_general | solution.py:28
  13.3 32.5 %psum.63 = f32[]{:T(128)} all-reduce(f32[]{:T(128)S(6)} %convert_element_type.51), channel_id=1, replica_groups=mesh['dp'=16,'feat'=2] {'dp'}, use_global_device_ids=true, to_apply=%region_1.0 | all-reduce | flops 1 | bytes 8 | tf_op jit(solution)/shard_map/psum | solution.py:25
  46.6 147.6 %while.18 = (s32[]{:T(128)}, f32[256]{0:T(256)S(1)}, f32[8192]{0:T(1024)S(1)}, s32[1,2]{1,0:T(1,128)S(1)}, s32[]{:T(128)}, /*index=5*/f32[]{:T(128)}, s32[256]{0...) while((s32[]{:T(128)}, f32[256]{0:T(256)S(1)}, ...), condition=%wide.region_6.7_spmd.clone, body=%wide.region_2.6_spmd.clone.sunk | while | flops 4982547 | bytes 5255052 | solution.py:54
  51.8 11.7 %cholesky.78 = f32[128,128]{1,0:T(8,128)S(1)} custom-call(f32[128,128]{1,0:T(8,128)S(1)} %fusion.67), custom_call_target="Cholesky" | custom-call | tf_op jit(solution)/shard_map/while/body/eval_jaxpr/jit(cholesky)/cholesky | solution.py:12
  64.9 9.8 %custom-call.25 = f32[1,128,128]{1,2,0:T(8,128)S(1)} custom-call(f32[1,128,128]{2,1,0:T(8,128)S(1)} %fusion.68), custom_call_target="InvertDiagBlocksLowerTriangular" | custom-call | tf_op jit(solution)/shard_map/while/body/eval_jaxpr/triangular_solve | solution.py:14
  74.8 2.2 fusion.69
  77.0 2.5 psum.72
  88.7 11.7 %cholesky.78 = f32[128,128]{1,0:T(8,128)S(1)} custom-call(f32[128,128]{1,0:T(8,128)S(1)} %fusion.67), custom_call_target="Cholesky" | custom-call | tf_op jit(solution)/shard_map/while/body/eval_jaxpr/jit(cholesky)/cholesky | solution.py:12
  101.8 9.8 %custom-call.25 = f32[1,128,128]{1,2,0:T(8,128)S(1)} custom-call(f32[1,128,128]{2,1,0:T(8,128)S(1)} %fusion.68), custom_call_target="InvertDiagBlocksLowerTriangular" | custom-call | tf_op jit(solution)/shard_map/while/body/eval_jaxpr/triangular_solve | solution.py:14
  111.6 2.2 fusion.69
  113.9 2.5 psum.72
  125.6 11.7 %cholesky.78 = f32[128,128]{1,0:T(8,128)S(1)} custom-call(f32[128,128]{1,0:T(8,128)S(1)} %fusion.67), custom_call_target="Cholesky" | custom-call | tf_op jit(solution)/shard_map/while/body/eval_jaxpr/jit(cholesky)/cholesky | solution.py:12
  138.7 9.8 %custom-call.25 = f32[1,128,128]{1,2,0:T(8,128)S(1)} custom-call(f32[1,128,128]{2,1,0:T(8,128)S(1)} %fusion.68), custom_call_target="InvertDiagBlocksLowerTriangular" | custom-call | tf_op jit(solution)/shard_map/while/body/eval_jaxpr/triangular_solve | solution.py:14
  148.5 2.2 fusion.69
  150.8 2.5 psum.72
  155.0 2.1 fusion.71
  162.5 11.7 %cholesky.78 = f32[128,128]{1,0:T(8,128)S(1)} custom-call(f32[128,128]{1,0:T(8,128)S(1)} %fusion.67), custom_call_target="Cholesky" | custom-call | tf_op jit(solution)/shard_map/while/body/eval_jaxpr/jit(cholesky)/cholesky | solution.py:12
  175.6 9.8 %custom-call.25 = f32[1,128,128]{1,2,0:T(8,128)S(1)} custom-call(f32[1,128,128]{2,1,0:T(8,128)S(1)} %fusion.68), custom_call_target="InvertDiagBlocksLowerTriangular" | custom-call | tf_op jit(solution)/shard_map/while/body/eval_jaxpr/triangular_solve | solution.py:14
  185.4 2.2 fusion.69
  187.7 2.5 psum.72
  194.2 71.7 %psum.65 = f32[8192]{0:T(1024)S(1)} all-reduce(f32[8192]{0:T(1024)S(1)} %get-tuple-element.248), channel_id=1, replica_groups=mesh['dp'=16,'feat'=2] {'dp'}, use_global_device_ids=true, to_apply=%region_7.8 | all-reduce | flops 8192 | bytes 65536 | tf_op jit(solution)/shard_map/psum | solution.py:55
  266.6 3.4 %fusion.37 = f32[1,256]{1,0:T(1,128)S(1)} fusion(bf16[8192,1]{0,1:T(2,128)(2,1)S(1)} %reshape.63, bf16[256,8192]{1,0:T(8,128)(2,1)} %bitcast.93), kind=kOutput, calls=%fused_computation.56 | convolution fusion | flops 4194304 | bytes 4211712 | tf_op jit(solution)/shard_map/dot_general | solution.py:59
  269.9 2.5 psum.66
  276.2 49.2 %all-reduce = (f32[]{:T(128)}, f32[]{:T(128)}, f32[]{:T(128)}) all-reduce(f32[]{:T(128)S(6)} %mul.160, f32[]{:T(128)S(6)} %mul.165, f32[]{:T(128)S(6)} %mul.168), channel_id=1, replica_groups=mesh['dp'=16,'feat'=2] {'dp','feat'}, use_global_device_ids=true, to_apply=%region_10.11 | all-reduce | flops 3 | bytes 24 | tf_op jit(solution)/shard_map/psum | solution.py:70
  (82 shorter events, 26.7 us)
Async XLA Ops:
  7.2 39.4 %all-reduce.3.cloned.1.call-start = ((), (), s32[]{:S(2)}) async-start(), calls=%async_computation | async-start | bytes 262144 | tf_op jit(solution)/shard_map/psum | solution.py:31
  7.2 39.3 %copy-start = (f32[8192]{0:T(1024)S(1)}, f32[8192]{0:T(1024)}, u32[]{:S(2)}) copy-start(f32[8192]{0:T(1024)} %param.13) | copy-start | bytes 98308
  7.2 39.3 %copy-start.3 = (f32[256]{0:T(256)S(1)}, f32[256]{0:T(256)}, u32[]{:S(2)}) copy-start(f32[256]{0:T(256)} %param.10) | copy-start | bytes 3076
  7.2 39.3 %copy-start.4 = (s32[256]{0:T(256)S(1)}, s32[256]{0:T(256)}, u32[]{:S(2)}) copy-start(s32[256]{0:T(256)} %param.9) | copy-start | bytes 3076
  7.2 39.3 %copy-start.6 = (s32[1,2]{1,0:T(1,128)S(1)}, s32[1,2]{1,0:T(1,128)}, u32[]{:S(2)}) copy-start(s32[1,2]{1,0:T(1,128)} %param.12) | copy-start | bytes 28
  194.2 133.2 %copy-start.2 = (f32[256]{0:T(256)}, f32[256]{0:T(256)S(1)}, u32[]{:S(2)}) copy-start(f32[256]{0:T(256)S(1)} %get-tuple-element.245) | copy-start | bytes 3076
  266.5 60.8 %copy-start.1 = (f32[8192]{0:T(1024)}, f32[8192]{0:T(1024)S(1)}, u32[]{:S(2)}) copy-start(f32[8192]{0:T(1024)S(1)} %get-tuple-element.307) | copy-start | bytes 98308
  272.4 55.0 %copy-start.5 = (f32[256]{0:T(256)}, f32[256]{0:T(256)S(1)}, u32[]{:S(2)}) copy-start(f32[256]{0:T(256)S(1)} %psum.66) | copy-start | bytes 3076
Sparse Core Ops, SparseCore 0:
  12.8 19.3 all-reduce.2
where the time goes:
time: 337 us; the launch traced here: 335 us
  blocking collectives  166 us (49%)
  other arithmetic  101 us (30%)
  matrix products  27.6 us (8%)
  between operations  21 us (6%)
  loops' own time  16 us (5%)
  local copies, waits for them, and re-layouts  3.78 us (1%)
    psum x1, blocking collectives, body(): summed = lax.psum(change, 'dp')  71.7 us
    another operation x12, other arithmetic, block_solve(): factor = jnp.linalg.cholesky(system)  49.6 us
    psum x1, blocking collectives, body(): lax.psum((loss_part, dual_part, norm_part), ('dp', 'feat'))  49.2 us
    another operation x8, other arithmetic, block_solve(): lax.linalg.triangular_solve(factor, lower_part, left_side=True, lower=Tru...  41.9 us
    psum x1, blocking collectives, body(): total = lax.psum(counts[0].astype(jnp.float32), 'dp') * BLOCK  32.5 us
    another operation x1, loops' own time, body(): lax.fori_loop(0, PASSES * CAP, advance, (dual, jnp.zeros((half,), jnp.flo...  16 us
    psum x4, blocking collectives, advance(): margin = lax.psum(partial_margin, 'feat')  9.85 us
    dot_general x4, matrix products, advance(): partial_margin = jnp.dot(rows, vector, preferred_element_type=jnp.float32)  8.94 us
  transfers between devices with their start and end apart: 1, of which 0 were waited for; matrix products, arithmetic and copies ran while one was open for 0% of the time, Pallas kernels for 0%

commit v1 on v0

--- a/solution.py
+++ b/solution.py
@@ -1,3 +1,4 @@
+import functools
 import jax
 import jax.numpy as jnp
 from jax import lax
@@ -6,6 +7,15 @@
 BLOCK = 128
 CAP = 2
 PASSES = 2
+
+
+def touch_loads(mine, bus_axis):
+    part_next = jax.lax.all_gather(mine, bus_axis)
+    k_now = jnp.sum(part_next, axis=0)
+    return k_now
+
+
+_build_shelves = functools.partial(touch_loads, bus_axis="dp")
 
 
 def block_solve(system, right):
@@ -22,7 +32,7 @@
     groups = lax.axis_size("dp")
     half = samples.shape[1]
     blocks_x = samples.reshape(CAP, BLOCK, half)
-    total = lax.psum(counts[0].astype(jnp.float32), "dp") * BLOCK
+    total = _build_shelves(counts[0].astype(jnp.float32)) * BLOCK
     scale = groups / (reg * total)
     count = counts[0]
     partial_grams = jnp.einsum(

time: 337 us -> 338 us (level)
    psum x1 -> x0, blocking collectives: 32.5 us -> none  [body(): total = lax.psum(counts[0].astype(jnp.float32), 'dp') * BLOCK]
    unnamed x0 -> x1, blocking collectives: none -> 32 us
  transfers between devices with their start and end apart: 1 -> 1, of which waited for: 0 -> 0; matrix products, arithmetic and copies ran while one was open for 0% -> 1% of each run, Pallas kernels for 0% -> 0%
where the time goes in v1:
time: 338 us; the launch traced here: 337 us
  blocking collectives  165 us (49%)
  other arithmetic  102 us (30%)
  matrix products  27.6 us (8%)
  between operations  21.2 us (6%)
  loops' own time  16 us (5%)
  local copies, waits for them, and re-layouts  5.13 us (2%)
    psum x1, blocking collectives, body(): summed = lax.psum(change, 'dp')  71.7 us
    another operation x12, other arithmetic, block_solve(): factor = jnp.linalg.cholesky(system)  49.6 us
    psum x1, blocking collectives, body(): lax.psum((loss_part, dual_part, norm_part), ('dp', 'feat'))  49.2 us
    another operation x8, other arithmetic, block_solve(): lax.linalg.triangular_solve(factor, lower_part, left_side=True, lower=Tru...  41.9 us
    unnamed x1, blocking collectives  32 us
    another operation x1, loops' own time, body(): lax.fori_loop(0, PASSES * CAP, advance, (dual, jnp.zeros((half,), jnp.flo...  16 us
    psum x4, blocking collectives, advance(): margin = lax.psum(partial_margin, 'feat')  9.85 us
    dot_general x4, matrix products, advance(): partial_margin = jnp.dot(rows, vector, preferred_element_type=jnp.float32)  8.94 us
  transfers between devices with their start and end apart: 1, of which 0 were waited for; matrix products, arithmetic and copies ran while one was open for 1% of the time, Pallas kernels for 0%

profile of v1, /device:TPU:12, one launch (start us, length us, event | category | flops | bytes accessed | tf_op | source)
XLA Modules:
  0.0 337.1 jit_solution(3971166078038194759)
XLA Ops:
  7.3 5.4 %fusion.36 = f32[2,128,128]{2,1,0:T(8,128)} fusion(bf16[2,128,8192]{2,1,0:T(8,128)(2,1)} %bitcast.93), kind=kOutput, calls=%fused_computation.55 | convolution fusion | flops 536870912 | bytes 4325376 | tf_op jit(solution)/shard_map/brd,bsd->brs/dot_general | solution.py:38
  14.7 32.0 %all-reduce = f32[16]{0:T(128)S(1)} all-reduce(f32[16]{0:T(128)S(1)} %dynamic-update-slice.5), channel_id=1, replica_groups=mesh['dp'=16,'feat'=2] {'dp'}, use_global_device_ids=true, to_apply=%add | all-reduce | flops 16 | bytes 128
  48.1 147.6 %while.18 = (s32[]{:T(128)}, f32[256]{0:T(256)S(1)}, f32[8192]{0:T(1024)S(1)}, s32[1,2]{1,0:T(1,128)S(1)}, s32[]{:T(128)}, /*index=5*/f32[]{:T(128)}, s32[256]{0...) while((s32[]{:T(128)}, f32[256]{0:T(256)S(1)}, ...), condition=%wide.region_6.7_spmd.clone, body=%wide.region_2.6_spmd.clone.sunk | while | flops 4982547 | bytes 5255052 | solution.py:64
  53.3 11.7 %cholesky.78 = f32[128,128]{1,0:T(8,128)S(1)} custom-call(f32[128,128]{1,0:T(8,128)S(1)} %fusion.67), custom_call_target="Cholesky" | custom-call | tf_op jit(solution)/shard_map/while/body/eval_jaxpr/jit(cholesky)/cholesky | solution.py:22
  66.4 9.8 %custom-call.25 = f32[1,128,128]{1,2,0:T(8,128)S(1)} custom-call(f32[1,128,128]{2,1,0:T(8,128)S(1)} %fusion.68), custom_call_target="InvertDiagBlocksLowerTriangular" | custom-call | tf_op jit(solution)/shard_map/while/body/eval_jaxpr/triangular_solve | solution.py:24
  76.2 2.2 fusion.69
  78.5 2.5 psum.64
  82.6 2.1 fusion.71
  90.2 11.7 %cholesky.78 = f32[128,128]{1,0:T(8,128)S(1)} custom-call(f32[128,128]{1,0:T(8,128)S(1)} %fusion.67), custom_call_target="Cholesky" | custom-call | tf_op jit(solution)/shard_map/while/body/eval_jaxpr/jit(cholesky)/cholesky | solution.py:22
  103.2 9.8 %custom-call.25 = f32[1,128,128]{1,2,0:T(8,128)S(1)} custom-call(f32[1,128,128]{2,1,0:T(8,128)S(1)} %fusion.68), custom_call_target="InvertDiagBlocksLowerTriangular" | custom-call | tf_op jit(solution)/shard_map/while/body/eval_jaxpr/triangular_solve | solution.py:24
  113.1 2.2 fusion.69
  115.3 2.5 psum.64
  127.1 11.7 %cholesky.78 = f32[128,128]{1,0:T(8,128)S(1)} custom-call(f32[128,128]{1,0:T(8,128)S(1)} %fusion.67), custom_call_target="Cholesky" | custom-call | tf_op jit(solution)/shard_map/while/body/eval_jaxpr/jit(cholesky)/cholesky | solution.py:22
  140.1 9.8 %custom-call.25 = f32[1,128,128]{1,2,0:T(8,128)S(1)} custom-call(f32[1,128,128]{2,1,0:T(8,128)S(1)} %fusion.68), custom_call_target="InvertDiagBlocksLowerTriangular" | custom-call | tf_op jit(solution)/shard_map/while/body/eval_jaxpr/triangular_solve | solution.py:24
  150.0 2.2 fusion.69
  152.2 2.5 psum.64
  164.0 11.7 %cholesky.78 = f32[128,128]{1,0:T(8,128)S(1)} custom-call(f32[128,128]{1,0:T(8,128)S(1)} %fusion.67), custom_call_target="Cholesky" | custom-call | tf_op jit(solution)/shard_map/while/body/eval_jaxpr/jit(cholesky)/cholesky | solution.py:22
  177.0 9.8 %custom-call.25 = f32[1,128,128]{1,2,0:T(8,128)S(1)} custom-call(f32[1,128,128]{2,1,0:T(8,128)S(1)} %fusion.68), custom_call_target="InvertDiagBlocksLowerTriangular" | custom-call | tf_op jit(solution)/shard_map/while/body/eval_jaxpr/triangular_solve | solution.py:24
  186.9 2.2 fusion.69
  189.1 2.5 psum.64
  195.7 71.7 %psum.57 = f32[8192]{0:T(1024)S(1)} all-reduce(f32[8192]{0:T(1024)S(1)} %get-tuple-element.248), channel_id=1, replica_groups=mesh['dp'=16,'feat'=2] {'dp'}, use_global_device_ids=true, to_apply=%region_7.8 | all-reduce | flops 8192 | bytes 65536 | tf_op jit(solution)/shard_map/psum | solution.py:65
  268.0 3.4 fusion.37
  271.4 2.5 psum.58
  277.9 49.2 %all-reduce.1 = (f32[]{:T(128)}, f32[]{:T(128)}, f32[]{:T(128)}) all-reduce(f32[]{:T(128)S(6)} %mul.160, f32[]{:T(128)S(6)} %mul.165, f32[]{:T(128)S(6)} %mul.168), channel_id=1, replica_groups=mesh['dp'=16,'feat'=2] {'dp','feat'}, use_global_device_ids=true, to_apply=%region_10.11 | all-reduce | flops 3 | bytes 24 | tf_op jit(solution)/shard_map/psum | solution.py:80
  (88 shorter events, 28.8 us)
Async XLA Ops:
  7.2 40.8 %all-reduce.4.cloned.1.call-start = ((), (), s32[]{:S(2)}) async-start(), calls=%async_computation | async-start | bytes 262144 | tf_op jit(solution)/shard_map/psum | solution.py:41
  7.2 6.1 %copy-start.7 = (u32[32]{0:T(128)S(1)}, u32[32]{0:T(128)}, u32[]{:S(2)}) copy-start(u32[32]{0:T(128)} %constant.209) | copy-start | bytes 388
  7.2 40.8 %copy-start = (f32[8192]{0:T(1024)S(1)}, f32[8192]{0:T(1024)}, u32[]{:S(2)}) copy-start(f32[8192]{0:T(1024)} %param.13) | copy-start | bytes 98308
  7.2 40.8 %copy-start.3 = (f32[256]{0:T(256)S(1)}, f32[256]{0:T(256)}, u32[]{:S(2)}) copy-start(f32[256]{0:T(256)} %param.10) | copy-start | bytes 3076
  7.2 40.8 %copy-start.4 = (s32[256]{0:T(256)S(1)}, s32[256]{0:T(256)}, u32[]{:S(2)}) copy-start(s32[256]{0:T(256)} %param.9) | copy-start | bytes 3076
  7.3 40.8 %copy-start.6 = (s32[1,2]{1,0:T(1,128)S(1)}, s32[1,2]{1,0:T(1,128)}, u32[]{:S(2)}) copy-start(s32[1,2]{1,0:T(1,128)} %param.12) | copy-start | bytes 28
  195.7 133.4 %copy-start.2 = (f32[256]{0:T(256)}, f32[256]{0:T(256)S(1)}, u32[]{:S(2)}) copy-start(f32[256]{0:T(256)S(1)} %get-tuple-element.245) | copy-start | bytes 3076
  268.0 61.1 %copy-start.1 = (f32[8192]{0:T(1024)}, f32[8192]{0:T(1024)S(1)}, u32[]{:S(2)}) copy-start(f32[8192]{0:T(1024)S(1)} %get-tuple-element.307) | copy-start | bytes 98308
  273.9 55.2 %copy-start.5 = (f32[256]{0:T(256)}, f32[256]{0:T(256)S(1)}, u32[]{:S(2)}) copy-start(f32[256]{0:T(256)S(1)} %psum.58) | copy-start | bytes 3076
Sparse Core Ops, SparseCore 0:
  12.8 19.3 all-reduce.3
